TPU v7x, 32 devices: a whole 2x2x4 slice. The times are simulated.
32 devices in a mesh: dp: 8 (over y, x, core), tp: 4 (over z).
Axes of the slice: x: 2, y: 2, z: 4, core: 2. Of those that a mesh axis runs over, the one named last changes fastest.
Arguments:
- inputs: bfloat16 [8, 768, 1280], P('dp', 'tp'), may hold values from -6 to 6
- saved_hidden: bfloat16 [8, 768, 5120], P('dp', None, 'tp'), may hold values from -8 to 8
- upstream: bfloat16 [8, 768, 1280], P('dp', 'tp'), may hold values from -6 to 6
- w_in: bfloat16 [1280, 5120], P(None, 'tp'), may hold values from -0.15625 to 0.15625
- w_out: bfloat16 [5120, 1280], P('tp'), may hold values from -0.078125 to 0.078125
- kernel: float32 [7, 1280], replicated, may hold values from -2 to 2
Outputs:
- grad_inputs: bfloat16 [8, 768, 1280], P('dp', 'tp')
- grad_w_in: float32 [1280, 5120], P(None, 'tp')
- grad_w_out: float32 [5120, 1280], P('tp')
- grad_bias: float32 [5120], P('tp')
- grad_kernel: float32 [7, 1280], replicated
All inputs are finite; a program needn't handle non-finite values.
Results may differ from a plain program's by a relative error of at most 0.02.
Values may be sent and summed in bfloat16 or wider, within the bound.
No kernel may reach another device: no remote copies, remote signals or barrier semaphores. Data moves between devices by JAX's collectives and lax.ppermute only.
A program may use at most 128 MiB of HBM per device.

v0:
```python
import jax
import jax.numpy as jnp
from jax import lax
from jax.sharding import PartitionSpec as P

KW = 7


def with_halo(cells, sides, width):
    for axis, dim in sides:
        count = lax.axis_size(axis)
        ends = count - 1
        head = lax.slice_in_dim(cells, 0, width, axis=dim)
        tail = lax.slice_in_dim(cells, cells.shape[dim] - width, cells.shape[dim], axis=dim)
        cells = jnp.concatenate(
            [
                lax.ppermute(tail, axis, [(i, (i + 1) % count) for i in range(ends)]),
                cells,
                lax.ppermute(head, axis, [((i + 1) % count, i) for i in range(ends)]),
            ],
            axis=dim,
        )
    return cells


def gelu_exact(value):
    return jax.nn.gelu(value, approximate=False)


def convolve(padded, kernel, length):
    mixed = padded[3 : 3 + length].astype(jnp.float32)
    for tap in range(KW):
        mixed = mixed + kernel[tap] * padded[tap : tap + length].astype(jnp.float32)
    return mixed.astype(jnp.bfloat16)


def shards(inputs, saved_hidden, upstream, w_in, w_out, kernel):
    tokens = inputs[0]
    hidden = saved_hidden[0]
    grad_out = upstream[0]
    length = tokens.shape[0]
    piece = lax.all_gather(grad_out, "tp", axis=0, tiled=True)
    hidden_rows = hidden.astype(jnp.float32)
    back_rows = lax.dot_general(
        piece, w_out, (((1,), (1,)), ((), ())), preferred_element_type=jnp.float32
    )
    grad_rows = jax.vjp(gelu_exact, hidden_rows)[1](back_rows)[0].astype(jnp.bfloat16)
    buffer = grad_rows
    activated = gelu_exact(hidden_rows).astype(jnp.bfloat16)
    total = lax.dot_general(
        activated, piece, (((0,), (0,)), ((), ())), preferred_element_type=jnp.float32
    )
    grad_w_out = total
    grad_bias = jnp.sum(buffer.astype(jnp.float32), axis=0)
    summed = lax.psum_scatter(
        lax.dot_general(
            buffer, w_in, (((1,), (1,)), ((), ())), preferred_element_type=jnp.float32
        ).astype(jnp.bfloat16),
        "tp",
        scatter_dimension=0,
        tiled=True,
    ).astype(jnp.float32)
    grad_mixed = (grad_out.astype(jnp.float32) + summed).astype(jnp.bfloat16)
    padded = with_halo(tokens, (("tp", 0),), 3)
    mixed = convolve(padded, kernel, length)
    grad_rows = buffer
    grad_w_in = lax.dot_general(
        lax.all_gather(mixed, "tp", axis=0, tiled=True),
        grad_rows,
        (((0,), (0,)), ((), ())),
        preferred_element_type=jnp.float32,
    )
    grad_pad = with_halo(grad_mixed, (("tp", 0),), 3)
    grad_f = grad_mixed.astype(jnp.float32)
    grad_inputs = grad_f
    taps = []
    for tap in range(KW):
        grad_inputs = grad_inputs + kernel[tap] * grad_pad[6 - tap : 6 - tap + length].astype(
            jnp.float32
        )
        taps.append(jnp.sum(grad_f * padded[tap : tap + length].astype(jnp.float32), axis=0))
    grad_kernel = jnp.stack(taps)
    grad_kernel = lax.psum(grad_kernel, ("dp", "tp"))
    grad_w_in, grad_w_out, grad_bias = (
        lax.psum(grad_w_in.astype(jnp.bfloat16), "dp").astype(jnp.float32),
        lax.psum(grad_w_out.astype(jnp.bfloat16), "dp").astype(jnp.float32),
        lax.psum(grad_bias.astype(jnp.bfloat16), "dp").astype(jnp.float32),
    )
    return (grad_inputs.astype(jnp.bfloat16)[None], grad_w_in, grad_w_out, grad_bias, grad_kernel)


def solution(mesh):
    in_specs = (
        P("dp", "tp", None),
        P("dp", None, "tp"),
        P("dp", "tp", None),
        P(None, "tp"),
        P("tp", None),
        P(),
    )
    out_specs = (P("dp", "tp", None), P(None, "tp"), P("tp", None), P("tp"), P())
    return jax.shard_map(shards, mesh=mesh, in_specs=in_specs, out_specs=out_specs, check_vma=False)
```

profile of v0, /device:TPU:0, one launch (start us, length us, event | category | flops | bytes accessed | tf_op | source)
XLA Modules:
  0.0 318.5 jit_solution(17866380397956469389)
XLA Ops:
  7.2 0.7 all-gather.6.cloned.1.call-update
  8.0 1.0 slice_bitcast_fusion.1
  8.9 5.0 %collective-permute-start.2 = (bf16[3,1280]{1,0:T(4,128)(2,1)S(1)}, bf16[3,1280]{1,0:T(4,128)(2,1)S(1)}, u32[]{:S(2)}, u32[]{:S(2)}) collective-permute-start(bf16[3,1280]{1,0:T(4,128)(2,1)S(1)} %get-tuple-element.27), channel_id=1, source_target_pairs={{0,1},{1,2},{2,3},{4,5},{5,6},{6,7},{8,9},{9,10},{10,11},{12,13},{... | collective-permute-start | bytes 23048 | tf_op jit(solution)/shard_map/ppermute | solution.py:17
  13.9 1.3 collective-permute-start.3
  15.2 1.3 slice_reduce_fusion.6
  16.5 3.0 collective-permute-done.3
  19.4 4.4 %fusion.52 = bf16[192,1280]{1,0:T(8,128)(2,1)} fusion(bf16[192,1280]{1,0:T(8,128)(2,1)} %bitcast.131, bf16[3,1280]{1,0:T(4,128)(2,1)S(1)} %collective-permute-done.3, bf16[3,1280]{1,0:T(4,128)(2,1)S(1)} %collective-permute-done.2, f32[1280]{0:T(1024)S(1)} %get-tuple-element.20, f32[1280]{0:T(1024)S(1)} %get-tuple-element.21, f32[1280]{0:T(1024)S(1)} %get-tuple-element.16, ...), kind=kLoop, calls=%fused_computation.72 | loop fusion | flops 9830400 | bytes 1034240 | tf_op jit(solution)/shard_map/convert_element_type | solution.py:34
  23.9 10.1 %fusion.38 = f32[768,1280]{1,0:T(8,128)} fusion(bf16[1,768,1280]{2,1,0:T(8,128)(2,1)} %param.7), kind=kLoop, calls=%fused_computation.43 | loop fusion | flops 61931520 | bytes 5898240 | tf_op jit(solution)/shard_map/jvp()/erfc | solution.py:27
  34.0 21.8 %all-gather.6.cloned.1.call-done = bf16[1,768,1280]{2,1,0:T(8,128)(2,1)} async-done(((bf16[1,192,1280]{2,1,0:T(8,128)(2,1)}), bf16[1,768,1280]{2,1,0:T(8,128)(2,1)}) %all-gather.6.cloned.1.call-update) | async-done | bytes 1966096 | tf_op jit(solution)/shard_map/all_gather | solution.py:42
  55.8 7.9 %convolution_convert_fusion = bf16[1280,1280]{1,0:T(8,128)(2,1)} fusion(f32[768,1280]{1,0:T(8,128)} %fusion.38, bf16[1,768,1280]{2,1,0:T(8,128)(2,1)} %param.7, bf16[1,768,1280]{2,1,0:T(8,128)(2,1)} %all-gather.6.cloned.1.call-done), kind=kOutput, calls=%fused_computation | convolution fusion | flops 2522152960 | bytes 11141120 | tf_op jit(solution)/shard_map/dot_general | solution.py:50
  63.8 4.7 %fusion.80 = (bf16[1280]{0:T(1024)(128)(2,1)S(1)}, bf16[768,1280]{1,0:T(8,128)(2,1)}) fusion(f32[768,1280]{1,0:T(8,128)S(1)} %copy-done.1, bf16[1280,1280]{1,0:T(8,128)(2,1)S(1)} %copy-done, bf16[1,768,1280]{2,1,0:T(8,128)(2,1)S(1)} %copy-done.5, bf16[1,768,1280]{2,1,0:T(8,128)(2,1)S(1)} %copy-done.4), kind=kOutput, calls=%fused_computation.121 | convolution fusion | flops 2532309760 | bytes 13109760 | tf_op jit(solution)/shard_map/dot_general | solution.py:44
  68.5 31.9 %all-gather.4.cloned.1.call-done = bf16[768,1280]{1,0:T(8,128)(2,1)} async-done(((bf16[192,1280]{1,0:T(8,128)(2,1)}), bf16[768,1280]{1,0:T(8,128)(2,1)}) %all-gather.4.cloned.1.call-update) | async-done | bytes 1966096 | tf_op jit(solution)/shard_map/all_gather | solution.py:68
  100.3 6.6 %convolution_convert_fusion.1 = bf16[1280,1280]{1,0:T(8,128)(2,1)} fusion(bf16[768,1280]{1,0:T(8,128)(2,1)} %all-gather.4.cloned.1.call-done, bf16[768,1280]{1,0:T(8,128)(2,1)} %get-tuple-element.30), kind=kOutput, calls=%fused_computation.1 | convolution fusion | flops 2518220800 | bytes 7208960 | tf_op jit(solution)/shard_map/dot_general | solution.py:67
  107.2 6.6 %convolution_convert_fusion.2 = bf16[768,1280]{1,0:T(8,128)(2,1)} fusion(bf16[768,1280]{1,0:T(8,128)(2,1)} %get-tuple-element.30, bf16[1280,1280]{1,0:T(8,128)(2,1)} %param.9), kind=kOutput, calls=%fused_computation.44 | convolution fusion | flops 2517565440 | bytes 7208960 | tf_op jit(solution)/shard_map/dot_general | solution.py:56
  113.8 14.3 %psum.30 = bf16[1280]{0:T(1024)(128)(2,1)S(1)} all-reduce(bf16[1280]{0:T(1024)(128)(2,1)S(1)} %get-tuple-element.29), channel_id=1, replica_groups=mesh['dp'=8,'tp'=4] {'dp'}, use_global_device_ids=true, to_apply=%region_4.0 | all-reduce | flops 1280 | bytes 5120 | tf_op jit(solution)/shard_map/psum | solution.py:87
  128.7 84.3 %all-reduce.3.cloned.1.call-done = (bf16[1280,1280]{1,0:T(8,128)(2,1)}, bf16[1280,1280]{1,0:T(8,128)(2,1)}) async-done(((bf16[1280,1280]{1,0:T(8,128)(2,1)}, bf16[1280,1280]{1,0:T(8,128)(2,1)}), (bf16[1280,1280]{1,0:T(8,128)(2,1)}, bf16[1280,1280]{1,0:T(8,128)(2,1)})) %all-reduce.3.cloned.1.call-update) | async-done | bytes 6553616 | tf_op jit(solution)/shard_map/psum | solution.py:85
  213.1 5.4 %convert_element_type.119 = f32[1280,1280]{1,0:T(8,128)} convert(bf16[1280,1280]{1,0:T(8,128)(2,1)} %get-tuple-element.22) | non-fusion elementwise | flops 1638400 | bytes 9830400 | tf_op jit(solution)/shard_map/convert_element_type | solution.py:85
  218.4 3.3 %convert_element_type.122 = f32[1280,1280]{1,0:T(8,128)} convert(bf16[1280,1280]{1,0:T(8,128)(2,1)S(1)} %copy-done.2) | non-fusion elementwise | flops 1638400 | bytes 9830400 | tf_op jit(solution)/shard_map/convert_element_type | solution.py:86
  221.7 35.3 %reduce-scatter.2.cloned.1.call-done = bf16[192,1280]{1,0:T(8,128)(2,1)} async-done(((bf16[768,1280]{1,0:T(8,128)(2,1)}), bf16[192,1280]{1,0:T(8,128)(2,1)}) %reduce-scatter.2.cloned.1.call-update) | async-done | bytes 491536 | tf_op jit(solution)/shard_map/reduce_scatter | solution.py:55
  257.0 3.8 %fusion.66 = (f32[1280]{0:T(1024)S(1)}, f32[1280]{0:T(1024)S(1)}, f32[1280]{0:T(1024)S(1)}, f32[1280]{0:T(1024)S(1)}, f32[1280]{0:T(1024)S(1)}, /*index=5*/f32[1...) fusion(bf16[3,1280]{1,0:T(4,128)(2,1)S(1)} %collective-permute-done.3, bf16[192,1280]{1,0:T(8,128)(2,1)} %bitcast.132, ...), kind=kLoop, calls=%fused_computation.86 | loop fusion | flops 10804480 | bytes 2508800 | tf_op jit(solution)/shard_map/reduce_sum | solution.py:81
  261.6 1.3 collective-permute-start
  262.9 4.5 %collective-permute-start.1 = (bf16[3,1280]{1,0:T(4,128)(2,1)S(1)}, bf16[3,1280]{1,0:T(4,128)(2,1)S(1)}, u32[]{:S(2)}, u32[]{:S(2)}) collective-permute-start(bf16[3,1280]{1,0:T(4,128)(2,1)S(1)} %get-tuple-element.26), channel_id=1, source_target_pairs={{0,1},{1,2},{2,3},{4,5},{5,6},{6,7},{8,9},{9,10},{10,11},{12,13},{... | collective-permute-start | bytes 23048 | tf_op jit(solution)/shard_map/ppermute | solution.py:17
  267.5 40.2 %psum.31 = f32[7,1280]{1,0:T(8,128)} all-reduce(f32[7,1280]{1,0:T(8,128)S(1)} %stack.31), channel_id=1, replica_groups=mesh['dp'=8,'tp'=4] {'dp','tp'}, use_global_device_ids=true, to_apply=%region_12.0 | all-reduce | flops 8960 | bytes 71680 | tf_op jit(solution)/shard_map/psum | solution.py:83
  307.6 4.3 %fusion.76 = bf16[1,192,1280]{2,1,0:T(8,128)(2,1)} fusion(bf16[192,1280]{1,0:T(8,128)(2,1)} %copy-done.3, bf16[3,1280]{1,0:T(4,128)(2,1)S(1)} %collective-permute-done.1, f32[1280]{0:T(1024)S(1)} %get-tuple-element.20, f32[1280]{0:T(1024)S(1)} %get-tuple-element.21, f32[1280]{0:T(1024)S(1)} %get-tuple-element.16, f32[1280]{0:T(1024)S(1)} %get-tuple-element.17, ...), kind=kLoop, calls=%fused_computation.109 | loop fusion | flops 9830400 | bytes 1034240 | tf_op jit(solution)/shard_map/broadcast_in_dim | solution.py:89
  (32 shorter events, 1.8 us)
Async XLA Ops:
  7.2 56.6 %copy-start = (bf16[1280,1280]{1,0:T(8,128)(2,1)S(1)}, bf16[1280,1280]{1,0:T(8,128)(2,1)}, u32[]{:S(2)}) copy-start(bf16[1280,1280]{1,0:T(8,128)(2,1)} %param.10) | copy-start | bytes 9830404
  7.2 48.6 %all-gather.6.cloned.1.call-start = ((), (), s32[]{:S(2)}) async-start(), calls=%async_computation.3 | async-start | bytes 2457600 | tf_op jit(solution)/shard_map/all_gather | solution.py:42
  7.9 92.4 %all-gather.4.cloned.1.call-start = ((), (), s32[]{:S(2)}) async-start(), calls=%async_computation.2 | async-start | bytes 2457600 | tf_op jit(solution)/shard_map/all_gather | solution.py:68
  8.9 7.5 %collective-permute-start.2 = (bf16[3,1280]{1,0:T(4,128)(2,1)S(1)}, bf16[3,1280]{1,0:T(4,128)(2,1)S(1)}, u32[]{:S(2)}, u32[]{:S(2)}) collective-permute-start(bf16[3,1280]{1,0:T(4,128)(2,1)S(1)} %get-tuple-element.27), channel_id=1, source_target_pairs={{0,1},{1,2},{2,3},{4,5},{5,6},{6,7},{8,9},{9,10},{10,11},{12,13},{... | collective-permute-start | bytes 23048 | tf_op jit(solution)/shard_map/ppermute | solution.py:17
  13.9 5.6 %collective-permute-start.3 = (bf16[3,1280]{1,0:T(4,128)(2,1)S(1)}, bf16[3,1280]{1,0:T(4,128)(2,1)S(1)}, u32[]{:S(2)}, u32[]{:S(2)}) collective-permute-start(bf16[3,1280]{1,0:T(4,128)(2,1)S(1)} %get-tuple-element.28), channel_id=1, source_target_pairs={{1,0},{2,1},{3,2},{5,4},{6,5},{7,6},{9,8},{10,9},{11,10},{13,12},{... | collective-permute-start | bytes 23048 | tf_op jit(solution)/shard_map/ppermute | solution.py:19
  23.9 189.2 %all-reduce.3.cloned.1.call-start = ((), (), s32[]{:S(2)}) async-start(), calls=%async_computation.4 | async-start | bytes 13107200 | tf_op jit(solution)/shard_map/psum | solution.py:85
  55.8 7.9 %copy-start.1 = (f32[768,1280]{1,0:T(8,128)S(1)}, f32[768,1280]{1,0:T(8,128)}, u32[]{:S(2)}) copy-start(f32[768,1280]{1,0:T(8,128)} %fusion.38) | copy-start | bytes 11796484
  55.8 7.9 %copy-start.4 = (bf16[1,768,1280]{2,1,0:T(8,128)(2,1)S(1)}, bf16[1,768,1280]{2,1,0:T(8,128)(2,1)}, u32[]{:S(2)}) copy-start(bf16[1,768,1280]{2,1,0:T(8,128)(2,1)} %param.7) | copy-start | bytes 5898244
  55.8 7.9 %copy-start.5 = (bf16[1,768,1280]{2,1,0:T(8,128)(2,1)S(1)}, bf16[1,768,1280]{2,1,0:T(8,128)(2,1)}, u32[]{:S(2)}) copy-start(bf16[1,768,1280]{2,1,0:T(8,128)(2,1)} %all-gather.6.cloned.1.call-done) | copy-start | bytes 5898244
  106.9 150.0 %reduce-scatter.2.cloned.1.call-start = ((), (), s32[]{:S(2)}) async-start(), calls=%async_computation.1 | async-start | bytes 2457600 | tf_op jit(solution)/shard_map/reduce_scatter | solution.py:55
  213.1 5.4 %copy-start.2 = (bf16[1280,1280]{1,0:T(8,128)(2,1)S(1)}, bf16[1280,1280]{1,0:T(8,128)(2,1)}, u32[]{:S(2)}) copy-start(bf16[1280,1280]{1,0:T(8,128)(2,1)} %get-tuple-element.23) | copy-start | bytes 9830404
  260.8 0.8 copy-start.3
  261.6 46.1 %collective-permute-start = (bf16[3,1280]{1,0:T(4,128)(2,1)S(1)}, bf16[3,1280]{1,0:T(4,128)(2,1)S(1)}, u32[]{:S(2)}, u32[]{:S(2)}) collective-permute-start(bf16[3,1280]{1,0:T(4,128)(2,1)S(1)} %get-tuple-element.25), channel_id=1, source_target_pairs={{1,0},{2,1},{3,2},{5,4},{6,5},{7,6},{9,8},{10,9},{11,10},{13,12},{... | collective-permute-start | bytes 23048 | tf_op jit(solution)/shard_map/ppermute | solution.py:19
  262.9 44.8 %collective-permute-start.1 = (bf16[3,1280]{1,0:T(4,128)(2,1)S(1)}, bf16[3,1280]{1,0:T(4,128)(2,1)S(1)}, u32[]{:S(2)}, u32[]{:S(2)}) collective-permute-start(bf16[3,1280]{1,0:T(4,128)(2,1)S(1)} %get-tuple-element.26), channel_id=1, source_target_pairs={{0,1},{1,2},{2,3},{4,5},{5,6},{6,7},{8,9},{9,10},{10,11},{12,13},{... | collective-permute-start | bytes 23048 | tf_op jit(solution)/shard_map/ppermute | solution.py:17
Sparse Core Ops, SparseCore 0:
  9.6 46.2 all-gather.5
  58.0 42.3 all-gather.3
  107.1 105.9 all-reduce.2
  215.2 41.6 reduce-scatter.1
where the time goes:
time: 319 us; the launch traced here: 318 us
  waiting for transfers between devices  177 us (55%)
  blocking collectives  54.5 us (17%)
  other arithmetic  31.8 us (10%)
  matrix products  25.8 us (8%)
  between operations  13.9 us (4%)
  starting transfers between devices  12.4 us (4%)
    psum x1, waiting for transfers between devices, shards(): lax.psum(grad_w_in.astype(jnp.bfloat16), 'dp').astype(jnp.float32)  84.3 us
    psum x1, blocking collectives, shards(): grad_kernel = lax.psum(grad_kernel, ('dp', 'tp'))  40.2 us
    reduce_scatter x1, waiting for transfers between devices, shards(): lax.psum_scatter(lax.dot_general(buffer, w_in, (((1,), (1,)), ((), ())),...  35.3 us
    all_gather x1, waiting for transfers between devices, shards(): lax.all_gather(mixed, 'tp', axis=0, tiled=True)  31.9 us
    all_gather x1, waiting for transfers between devices, shards(): piece = lax.all_gather(grad_out, 'tp', axis=0, tiled=True)  21.8 us
    psum x1, blocking collectives, shards(): lax.psum(grad_bias.astype(jnp.bfloat16), 'dp').astype(jnp.float32)  14.3 us
    another operation x1, other arithmetic, gelu_exact(): return jax.nn.gelu(value, approximate=False)  10.1 us
    ppermute x2, starting transfers between devices, with_halo(): lax.ppermute(tail, axis, [(i, (i + 1) % count) for i in range(ends)])  9.5 us
  transfers between devices with their start and end apart: 8, of which 5 were waited for; matrix products, arithmetic and copies ran while one was open for 14% of the time, Pallas kernels for 0%

commit v1 on v0

--- a/solution.py
+++ b/solution.py
@@ -39,7 +39,12 @@
     hidden = saved_hidden[0]
     grad_out = upstream[0]
     length = tokens.shape[0]
-    piece = lax.all_gather(grad_out, "tp", axis=0, tiled=True)
+    ring = [grad_out]
+    for hop in range(3):
+        ring.append(lax.ppermute(ring[-1], "tp", [(dev, (dev + 1) % 4) for dev in range(4)]))
+    piece = jnp.roll(
+        jnp.concatenate(ring[::-1], axis=0), (lax.axis_index("tp") + 1) * ring[0].shape[0], axis=0
+    )
     hidden_rows = hidden.astype(jnp.float32)
     back_rows = lax.dot_general(
         piece, w_out, (((1,), (1,)), ((), ())), preferred_element_type=jnp.float32

time: 319 us -> 257 us (0.81)
  waiting for transfers between devices: 177 us -> 108 us
  local copies, waits for them, and re-layouts: 3.03 us -> 10.5 us
  matrix products: 25.8 us -> 22.3 us
    psum x1, waiting for transfers between devices: 84.3 us -> 54.8 us  [shards(): lax.psum(grad_w_in.astype(jnp.bfloat16), 'dp').astype(jnp.float32)]
    all_gather x1 -> x0, waiting for transfers between devices: 21.8 us -> none  [shards(): piece = lax.all_gather(grad_out, 'tp', axis=0, tiled=True)]
    ppermute x0 -> x3, waiting for transfers between devices: none -> 21.4 us  [shards(): lax.ppermute(ring[-1], 'tp', [(dev, (dev + 1) % 4) for dev in range(4)])]
    all_gather x1, waiting for transfers between devices: 31.9 us -> 10.9 us  [shards(): lax.all_gather(mixed, 'tp', axis=0, tiled=True)]
    reduce_scatter x1, waiting for transfers between devices: 35.3 us -> 21.3 us  [shards(): lax.psum_scatter(lax.dot_general(buffer, w_in, (((1,), (1,)), ((), ())),...]
    unnamed x12 -> x27, local copies, waits for them, and re-layouts: 0.7 us -> 9.51 us
  transfers between devices with their start and end apart: 8 -> 10, of which waited for: 5 -> 6; matrix products, arithmetic and copies ran while one was open for 14% -> 21% of each run, Pallas kernels for 0% -> 0%
where the time goes in v1:
time: 257 us
  waiting for transfers between devices  108 us (42%)
  blocking collectives  55.3 us (22%)
  other arithmetic  32.2 us (13%)
  matrix products  22.3 us (9%)
  starting transfers between devices  14 us (5%)
  between operations  14 us (5%)
  local copies, waits for them, and re-layouts  10.5 us (4%)
    psum x1, waiting for transfers between devices, shards(): lax.psum(grad_w_in.astype(jnp.bfloat16), 'dp').astype(jnp.float32)  54.8 us
    psum x1, blocking collectives, shards(): grad_kernel = lax.psum(grad_kernel, ('dp', 'tp'))  41.1 us
    ppermute x3, waiting for transfers between devices, shards(): lax.ppermute(ring[-1], 'tp', [(dev, (dev + 1) % 4) for dev in range(4)])  21.4 us
    reduce_scatter x1, waiting for transfers between devices, shards(): lax.psum_scatter(lax.dot_general(buffer, w_in, (((1,), (1,)), ((), ())),...  21.3 us
    psum x1, blocking collectives, shards(): lax.psum(grad_bias.astype(jnp.bfloat16), 'dp').astype(jnp.float32)  14.2 us
    all_gather x1, waiting for transfers between devices, shards(): lax.all_gather(mixed, 'tp', axis=0, tiled=True)  10.9 us
    another operation x1, other arithmetic, gelu_exact(): return jax.nn.gelu(value, approximate=False)  10.1 us
    unnamed x27, local copies, waits for them, and re-layouts  9.51 us
  transfers between devices with their start and end apart: 10, of which 6 were waited for; matrix products, arithmetic and copies ran while one was open for 21% of the time, Pallas kernels for 0%

profile of v1, /device:TPU:0, one launch (start us, length us, event | category | flops | bytes accessed | tf_op | source)
XLA Modules:
  0.0 256.8 jit_solution(11554418461380868126)
XLA Ops:
  7.2 3.1 %collective-permute-start = (bf16[192,1280]{1,0:T(8,128)(2,1)}, bf16[192,1280]{1,0:T(8,128)(2,1)}, u32[]{:S(2)}, u32[]{:S(2)}) collective-permute-start(bf16[192,1280]{1,0:T(8,128)(2,1)} %bitcast.125), channel_id=1, source_target_pairs={{0,1},{1,2},{2,3},{3,0},{4,5},{5,6},{6,7},{7,4},{8,9},{9,10},{10,1... | collective-permute-start | bytes 1474568 | tf_op jit(solution)/shard_map/ppermute | solution.py:44
  11.1 3.5 %collective-permute-start.5 = (bf16[3,1280]{1,0:T(4,128)(2,1)S(1)}, bf16[3,1280]{1,0:T(4,128)(2,1)S(1)}, u32[]{:S(2)}, u32[]{:S(2)}) collective-permute-start(bf16[3,1280]{1,0:T(4,128)(2,1)S(1)} %get-tuple-element.27), channel_id=1, source_target_pairs={{0,1},{1,2},{2,3},{4,5},{5,6},{6,7},{8,9},{9,10},{10,11},{12,13},{... | collective-permute-start | bytes 23048 | tf_op jit(solution)/shard_map/ppermute | solution.py:17
  14.6 1.3 collective-permute-start.6
  15.9 8.2 %collective-permute-done = bf16[192,1280]{1,0:T(8,128)(2,1)} collective-permute-done((bf16[192,1280]{1,0:T(8,128)(2,1)}, bf16[192,1280]{1,0:T(8,128)(2,1)}, u32[]{:S(2)}, u32[]{:S(2)}) %collective-permute-start) | collective-permute-done | bytes 491552 | tf_op jit(solution)/shard_map/ppermute | solution.py:44
  24.1 10.1 %fusion.38 = f32[768,1280]{1,0:T(8,128)} fusion(bf16[1,768,1280]{2,1,0:T(8,128)(2,1)} %param.7), kind=kLoop, calls=%fused_computation.43 | loop fusion | flops 61931520 | bytes 5898240 | tf_op jit(solution)/shard_map/jvp()/erfc | solution.py:27
  34.3 4.2 %collective-permute-done.1 = bf16[192,1280]{1,0:T(8,128)(2,1)} collective-permute-done((bf16[192,1280]{1,0:T(8,128)(2,1)}, bf16[192,1280]{1,0:T(8,128)(2,1)}, u32[]{:S(2)}, u32[]{:S(2)}) %collective-permute-start.1) | collective-permute-done | bytes 491552 | tf_op jit(solution)/shard_map/ppermute | solution.py:44
  38.5 4.4 %fusion.52 = bf16[192,1280]{1,0:T(8,128)(2,1)} fusion(bf16[192,1280]{1,0:T(8,128)(2,1)} %bitcast.123, bf16[3,1280]{1,0:T(4,128)(2,1)S(1)} %collective-permute-done.6, bf16[3,1280]{1,0:T(4,128)(2,1)S(1)} %collective-permute-done.5, f32[1280]{0:T(1024)S(1)} %get-tuple-element.20, f32[1280]{0:T(1024)S(1)} %get-tuple-element.21, f32[1280]{0:T(1024)S(1)} %get-tuple-element.16, ...), kind=kLoop, calls=%fused_computation.72 | loop fusion | flops 9830400 | bytes 1034240 | tf_op jit(solution)/shard_map/convert_element_type | solution.py:34
  43.0 9.0 %collective-permute-done.2 = bf16[192,1280]{1,0:T(8,128)(2,1)} collective-permute-done((bf16[192,1280]{1,0:T(8,128)(2,1)}, bf16[192,1280]{1,0:T(8,128)(2,1)}, u32[]{:S(2)}, u32[]{:S(2)}) %collective-permute-start.2) | collective-permute-done | bytes 491552 | tf_op jit(solution)/shard_map/ppermute | solution.py:44
  59.6 3.9 %fusion.80 = (bf16[1280]{0:T(1024)(128)(2,1)S(1)}, bf16[768,1280]{1,0:T(8,128)(2,1)S(1)}) fusion(f32[768,1280]{1,0:T(8,128)S(1)} %copy-done.2, bf16[1280,1280]{1,0:T(8,128)(2,1)S(1)} %copy-done, bf16[1536,1280]{1,0:T(8,128)(2,1)S(1)} %constant_dynamic-update-slice_fusion, s32[]{:T(128)S(6)} %select_n.14, bf16[1,768,1280]{2,1,0:T(8,128)(2,1)S(1)} %copy-done.5), kind=kOutput, calls=%fused_computation.130 | convolution fusion | flops 2532309760 | bytes 13109764 | tf_op jit(solution)/shard_map/dot_general | solution.py:49
  63.5 1.3 copy-done.9
  64.8 3.9 %convolution_convert_fusion.2 = bf16[768,1280]{1,0:T(8,128)(2,1)} fusion(bf16[768,1280]{1,0:T(8,128)(2,1)S(1)} %get-tuple-element.30, bf16[1280,1280]{1,0:T(8,128)(2,1)S(1)} %copy-done.8), kind=kOutput, calls=%fused_computation.44 | convolution fusion | flops 2517565440 | bytes 7208960 | tf_op jit(solution)/shard_map/dot_general | solution.py:61
  69.0 7.9 %convolution_convert_fusion = bf16[1280,1280]{1,0:T(8,128)(2,1)} fusion(f32[768,1280]{1,0:T(8,128)} %fusion.38, bf16[1,768,1280]{2,1,0:T(8,128)(2,1)} %param.7, bf16[1536,1280]{1,0:T(8,128)(2,1)} %copy-done.6, s32[]{:T(128)S(6)} %select_n.14), kind=kOutput, calls=%fused_computation | convolution fusion | flops 2522152960 | bytes 11141124 | tf_op jit(solution)/shard_map/dot_general | solution.py:55
  76.9 10.9 %all-gather.2.cloned.1.call-done = bf16[768,1280]{1,0:T(8,128)(2,1)} async-done(((bf16[192,1280]{1,0:T(8,128)(2,1)}), bf16[768,1280]{1,0:T(8,128)(2,1)}) %all-gather.2.cloned.1.call-update) | async-done | bytes 1966096 | tf_op jit(solution)/shard_map/all_gather | solution.py:73
  87.8 6.6 %convolution_convert_fusion.1 = bf16[1280,1280]{1,0:T(8,128)(2,1)} fusion(bf16[768,1280]{1,0:T(8,128)(2,1)} %all-gather.2.cloned.1.call-done, bf16[768,1280]{1,0:T(8,128)(2,1)} %copy-done.9), kind=kOutput, calls=%fused_computation.1 | convolution fusion | flops 2518220800 | bytes 7208960 | tf_op jit(solution)/shard_map/dot_general | solution.py:72
  94.4 14.2 %psum.30 = bf16[1280]{0:T(1024)(128)(2,1)S(1)} all-reduce(bf16[1280]{0:T(1024)(128)(2,1)S(1)} %get-tuple-element.29), channel_id=1, replica_groups=mesh['dp'=8,'tp'=4] {'dp'}, use_global_device_ids=true, to_apply=%region_4.5 | all-reduce | flops 1280 | bytes 5120 | tf_op jit(solution)/shard_map/psum | solution.py:92
  109.2 21.3 %reduce-scatter.2.cloned.1.call-done = bf16[192,1280]{1,0:T(8,128)(2,1)} async-done(((bf16[768,1280]{1,0:T(8,128)(2,1)}), bf16[192,1280]{1,0:T(8,128)(2,1)}) %reduce-scatter.2.cloned.1.call-update) | async-done | bytes 491536 | tf_op jit(solution)/shard_map/reduce_scatter | solution.py:60
  130.5 3.8 %fusion.66 = (f32[1280]{0:T(1024)S(1)}, f32[1280]{0:T(1024)S(1)}, f32[1280]{0:T(1024)S(1)}, f32[1280]{0:T(1024)S(1)}, f32[1280]{0:T(1024)S(1)}, /*index=5*/f32[1...) fusion(bf16[3,1280]{1,0:T(4,128)(2,1)S(1)} %collective-permute-done.6, bf16[192,1280]{1,0:T(8,128)(2,1)} %bitcast.124, ...), kind=kLoop, calls=%fused_computation.86 | loop fusion | flops 10804480 | bytes 2508800 | tf_op jit(solution)/shard_map/reduce_sum | solution.py:86
  135.1 1.3 collective-permute-start.3
  136.4 4.5 %collective-permute-start.4 = (bf16[3,1280]{1,0:T(4,128)(2,1)S(1)}, bf16[3,1280]{1,0:T(4,128)(2,1)S(1)}, u32[]{:S(2)}, u32[]{:S(2)}) collective-permute-start(bf16[3,1280]{1,0:T(4,128)(2,1)S(1)} %get-tuple-element.26), channel_id=1, source_target_pairs={{0,1},{1,2},{2,3},{4,5},{5,6},{6,7},{8,9},{9,10},{10,11},{12,13},{... | collective-permute-start | bytes 23048 | tf_op jit(solution)/shard_map/ppermute | solution.py:17
  141.0 41.1 %psum.31 = f32[7,1280]{1,0:T(8,128)} all-reduce(f32[7,1280]{1,0:T(8,128)S(1)} %stack.31), channel_id=1, replica_groups=mesh['dp'=8,'tp'=4] {'dp','tp'}, use_global_device_ids=true, to_apply=%region_12.13 | all-reduce | flops 8960 | bytes 71680 | tf_op jit(solution)/shard_map/psum | solution.py:88
  182.1 4.7 %fusion.75 = bf16[1,192,1280]{2,1,0:T(8,128)(2,1)} fusion(bf16[192,1280]{1,0:T(8,128)(2,1)} %copy-done.4, bf16[3,1280]{1,0:T(4,128)(2,1)S(1)} %collective-permute-done.4, f32[1280]{0:T(1024)S(1)} %get-tuple-element.20, f32[1280]{0:T(1024)S(1)} %get-tuple-element.21, f32[1280]{0:T(1024)S(1)} %get-tuple-element.16, f32[1280]{0:T(1024)S(1)} %get-tuple-element.17, ...), kind=kLoop, calls=%fused_computation.108 | loop fusion | flops 9830400 | bytes 1034240 | tf_op jit(solution)/shard_map/broadcast_in_dim | solution.py:94
  186.8 54.8 %all-reduce.3.cloned.1.call-done = (bf16[1280,1280]{1,0:T(8,128)(2,1)}, bf16[1280,1280]{1,0:T(8,128)(2,1)}) async-done(((bf16[1280,1280]{1,0:T(8,128)(2,1)}, bf16[1280,1280]{1,0:T(8,128)(2,1)}), (bf16[1280,1280]{1,0:T(8,128)(2,1)}, bf16[1280,1280]{1,0:T(8,128)(2,1)})) %all-reduce.3.cloned.1.call-update) | async-done | bytes 6553616 | tf_op jit(solution)/shard_map/psum | solution.py:90
  241.6 5.4 %convert_element_type.119 = f32[1280,1280]{1,0:T(8,128)} convert(bf16[1280,1280]{1,0:T(8,128)(2,1)} %get-tuple-element.22) | non-fusion elementwise | flops 1638400 | bytes 9830400 | tf_op jit(solution)/shard_map/convert_element_type | solution.py:90
  247.0 3.3 %convert_element_type.122 = f32[1280,1280]{1,0:T(8,128)} convert(bf16[1280,1280]{1,0:T(8,128)(2,1)S(1)} %copy-done.3) | non-fusion elementwise | flops 1638400 | bytes 9830400 | tf_op jit(solution)/shard_map/convert_element_type | solution.py:91
  (51 shorter events, 10.2 us)
Async XLA Ops:
  7.2 52.4 %copy-start = (bf16[1280,1280]{1,0:T(8,128)(2,1)S(1)}, bf16[1280,1280]{1,0:T(8,128)(2,1)}, u32[]{:S(2)}) copy-start(bf16[1280,1280]{1,0:T(8,128)(2,1)} %param.10) | copy-start | bytes 9830404
  7.2 27.0 %copy-start.7 = (f32[7,1280]{1,0:T(8,128)S(1)}, f32[7,1280]{1,0:T(8,128)}, u32[]{:S(2)}) copy-start(f32[7,1280]{1,0:T(8,128)} %param.11) | copy-start | bytes 107524
  7.2 80.6 %all-gather.2.cloned.1.call-start = ((), (), s32[]{:S(2)}) async-start(), calls=%async_computation.2 | async-start | bytes 2457600 | tf_op jit(solution)/shard_map/all_gather | solution.py:73
  7.2 16.8 %collective-permute-start = (bf16[192,1280]{1,0:T(8,128)(2,1)}, bf16[192,1280]{1,0:T(8,128)(2,1)}, u32[]{:S(2)}, u32[]{:S(2)}) collective-permute-start(bf16[192,1280]{1,0:T(8,128)(2,1)} %bitcast.125), channel_id=1, source_target_pairs={{0,1},{1,2},{2,3},{3,0},{4,5},{5,6},{6,7},{7,4},{8,9},{9,10},{10,1... | collective-permute-start | bytes 1474568 | tf_op jit(solution)/shard_map/ppermute | solution.py:44
  11.1 27.4 %collective-permute-start.5 = (bf16[3,1280]{1,0:T(4,128)(2,1)S(1)}, bf16[3,1280]{1,0:T(4,128)(2,1)S(1)}, u32[]{:S(2)}, u32[]{:S(2)}) collective-permute-start(bf16[3,1280]{1,0:T(4,128)(2,1)S(1)} %get-tuple-element.27), channel_id=1, source_target_pairs={{0,1},{1,2},{2,3},{4,5},{5,6},{6,7},{8,9},{9,10},{10,11},{12,13},{... | collective-permute-start | bytes 23048 | tf_op jit(solution)/shard_map/ppermute | solution.py:17
  14.6 23.9 %collective-permute-start.6 = (bf16[3,1280]{1,0:T(4,128)(2,1)S(1)}, bf16[3,1280]{1,0:T(4,128)(2,1)S(1)}, u32[]{:S(2)}, u32[]{:S(2)}) collective-permute-start(bf16[3,1280]{1,0:T(4,128)(2,1)S(1)} %get-tuple-element.28), channel_id=1, source_target_pairs={{1,0},{2,1},{3,2},{5,4},{6,5},{7,6},{9,8},{10,9},{11,10},{13,12},{... | collective-permute-start | bytes 23048 | tf_op jit(solution)/shard_map/ppermute | solution.py:19
  24.1 14.4 %collective-permute-start.1 = (bf16[192,1280]{1,0:T(8,128)(2,1)}, bf16[192,1280]{1,0:T(8,128)(2,1)}, u32[]{:S(2)}, u32[]{:S(2)}) collective-permute-start(bf16[192,1280]{1,0:T(8,128)(2,1)} %collective-permute-done), channel_id=1, source_target_pairs={{0,1},{1,2},{2,3},{3,0},{4,5},{5,6},{6,7},{7,4},{8,9},{9,10},{10,1... | collective-permute-start | bytes 1474568 | tf_op jit(solution)/shard_map/ppermute | solution.py:44
  38.5 13.5 %collective-permute-start.2 = (bf16[192,1280]{1,0:T(8,128)(2,1)}, bf16[192,1280]{1,0:T(8,128)(2,1)}, u32[]{:S(2)}, u32[]{:S(2)}) collective-permute-start(bf16[192,1280]{1,0:T(8,128)(2,1)} %collective-permute-done.1), channel_id=1, source_target_pairs={{0,1},{1,2},{2,3},{3,0},{4,5},{5,6},{6,7},{7,4},{8,9},{9,10},{10,1... | collective-permute-start | bytes 1474568 | tf_op jit(solution)/shard_map/ppermute | solution.py:44
  42.9 87.7 %reduce-scatter.2.cloned.1.call-start = ((), (), s32[]{:S(2)}) async-start(), calls=%async_computation.1 | async-start | bytes 2457600 | tf_op jit(solution)/shard_map/reduce_scatter | solution.py:60
  42.9 16.6 %copy-start.1 = (bf16[1,192,1280]{2,1,0:T(8,128)(2,1)S(1)}, bf16[1,192,1280]{2,1,0:T(8,128)(2,1)}, u32[]{:S(2)}) copy-start(bf16[1,192,1280]{2,1,0:T(8,128)(2,1)} %param.8) | copy-start | bytes 1474564
  42.9 16.6 %copy-start.2 = (f32[768,1280]{1,0:T(8,128)S(1)}, f32[768,1280]{1,0:T(8,128)}, u32[]{:S(2)}) copy-start(f32[768,1280]{1,0:T(8,128)} %fusion.38) | copy-start | bytes 11796484
  42.9 16.6 %copy-start.5 = (bf16[1,768,1280]{2,1,0:T(8,128)(2,1)S(1)}, bf16[1,768,1280]{2,1,0:T(8,128)(2,1)}, u32[]{:S(2)}) copy-start(bf16[1,768,1280]{2,1,0:T(8,128)(2,1)} %param.7) | copy-start | bytes 5898244
  59.6 3.9 %copy-start.6 = (bf16[1536,1280]{1,0:T(8,128)(2,1)}, bf16[1536,1280]{1,0:T(8,128)(2,1)S(1)}, u32[]{:S(2)}) copy-start(bf16[1536,1280]{1,0:T(8,128)(2,1)S(1)} %constant_dynamic-update-slice_fusion) | copy-start | bytes 11796484
  59.6 5.2 %copy-start.8 = (bf16[1280,1280]{1,0:T(8,128)(2,1)S(1)}, bf16[1280,1280]{1,0:T(8,128)(2,1)}, u32[]{:S(2)}) copy-start(bf16[1280,1280]{1,0:T(8,128)(2,1)} %param.9) | copy-start | bytes 9830404
  63.5 1.3 copy-start.9
  68.8 172.8 %all-reduce.3.cloned.1.call-start = ((), (), s32[]{:S(2)}) async-start(), calls=%async_computation.3 | async-start | bytes 13107200 | tf_op jit(solution)/shard_map/psum | solution.py:90
  134.3 0.8 copy-start.4
  135.1 47.0 %collective-permute-start.3 = (bf16[3,1280]{1,0:T(4,128)(2,1)S(1)}, bf16[3,1280]{1,0:T(4,128)(2,1)S(1)}, u32[]{:S(2)}, u32[]{:S(2)}) collective-permute-start(bf16[3,1280]{1,0:T(4,128)(2,1)S(1)} %get-tuple-element.25), channel_id=1, source_target_pairs={{1,0},{2,1},{3,2},{5,4},{6,5},{7,6},{9,8},{10,9},{11,10},{13,12},{... | collective-permute-start | bytes 23048 | tf_op jit(solution)/shard_map/ppermute | solution.py:19
  136.4 45.7 %collective-permute-start.4 = (bf16[3,1280]{1,0:T(4,128)(2,1)S(1)}, bf16[3,1280]{1,0:T(4,128)(2,1)S(1)}, u32[]{:S(2)}, u32[]{:S(2)}) collective-permute-start(bf16[3,1280]{1,0:T(4,128)(2,1)S(1)} %get-tuple-element.26), channel_id=1, source_target_pairs={{0,1},{1,2},{2,3},{4,5},{5,6},{6,7},{8,9},{9,10},{10,11},{12,13},{... | collective-permute-start | bytes 23048 | tf_op jit(solution)/shard_map/ppermute | solution.py:17
  241.6 5.4 %copy-start.3 = (bf16[1280,1280]{1,0:T(8,128)(2,1)S(1)}, bf16[1280,1280]{1,0:T(8,128)(2,1)}, u32[]{:S(2)}) copy-start(bf16[1280,1280]{1,0:T(8,128)(2,1)} %get-tuple-element.23) | copy-start | bytes 9830404
Sparse Core Ops, SparseCore 0:
  43.0 44.7 all-gather.1
  90.1 40.4 reduce-scatter.1
  134.5 107.0 all-reduce.2
